TPU v7x, 256 devices: a whole 4x4x8 slice. The times are simulated.
256 devices in a mesh: seq: 8 (over y, x_lo), blk: 32 (over z, x_hi, core).
Axes of the slice: x: 4 (x_hi: 2, x_lo: 2; x = x_hi * 2 + x_lo), y: 4, z: 8, core: 2. Of those that a mesh axis runs over, the one named last changes fastest.
Arguments:
- activations: bfloat16 [2, 64, 1024, 4096], P(None, 'blk', 'seq'), may hold values from -120 to 120, as said below
- out_grads: bfloat16 [2, 64, 1024, 4096], P(None, 'blk', 'seq'), may hold values from -120 to 120, as said below
- lengths: int32 [64], P('blk'), may hold values from 512 to 1024
- input_proj: bfloat16 [2, 64, 4096], replicated, may hold values from -0.09375 to 0.09375
- output_proj: bfloat16 [2, 64, 4096], replicated, may hold values from -0.09375 to 0.09375
- stored_proj: float32 [16384, 2, 64, 64], P(('seq', 'blk')), may hold values from -6 to 6
Outputs:
- scores: float32 [64, 16384], P('blk', 'seq')
Inputs may be any that keep to these rules, and one draw needn't show every extreme that they name: `activations`: finite values. `out_grads`: finite values.
All inputs are finite; a program needn't handle non-finite values.
Results may differ from a plain program's by a relative error of at most 0.0003.
Values sent between devices are 32-bit elements; how exact they have to be, the bound alone decides.
No kernel may reach another device: no remote copies, remote signals or barrier semaphores. Data moves between devices by JAX's collectives and lax.ppermute only.
A program may use at most 64 MiB of HBM per device.

v0:
```python
import functools
import math

import jax
import jax.numpy as jnp
from jax import lax
from jax.experimental import pallas as pl
from jax.experimental.pallas import tpu as pltpu
from jax.sharding import Mesh, PartitionSpec as P


damping = 0.1
SEQ = ("y", "x_lo")
BLK = ("z", "x_hi", "core")
HALF = 64
WIDE = 128
f32 = jnp.float32
bf16 = jnp.bfloat16
NT = (((1,), (1,)), ((), ()))
NN = (((1,), (0,)), ((), ()))


def cost(flops, moved):
    return pl.CostEstimate(flops=flops, bytes_accessed=moved, transcendentals=0)


def lanes_of(shape):
    return lax.broadcasted_iota(jnp.int32, shape, len(shape) - 1)


def in_two(x):
    high = x.astype(bf16)
    return high, (x - high.astype(f32)).astype(bf16)


def three_pass(a, b, dims):
    dot = functools.partial(lax.dot_general, dimension_numbers=dims, preferred_element_type=f32)
    rows = a[0].shape[0]
    stacked = dot(jnp.concatenate(a, axis=0), b[0])
    return stacked[:rows] + (stacked[rows:] + dot(a[0], b[1]))


def project_kernel(length_ref, start_ref, act_hbm, grad_hbm, win_hbm, wout_hbm, out_ref, act, grad, win, wout, sems):
    layers, rolls, seq, width = act.shape
    cuts = sems.shape[2]
    depth = width // cuts
    sides = ((act_hbm, act, win_hbm, win), (grad_hbm, grad, wout_hbm, wout))

    def copies(l, side, k):
        big_from, big_to, weight_from, weight_to = sides[side]
        span = pl.ds(k * depth, depth)
        return (
            pltpu.make_async_copy(weight_from.at[l, :, span], weight_to.at[l, :, span], sems.at[l, side, k, 0]),
            pltpu.make_async_copy(
                big_from.at[l, :, :, span], big_to.at[l, :, :, span], sems.at[l, side, k, 1]
            ),
        )

    every = [(l, side, k) for l in range(layers) for k in range(cuts) for side in range(2)]
    for place in every:
        for copy in copies(*place):
            copy.start()
    dot = functools.partial(lax.dot_general, dimension_numbers=NT, preferred_element_type=f32)
    lane = lanes_of((HALF, WIDE))
    row = lax.broadcasted_iota(jnp.int32, (HALF, WIDE), 0)
    position = lax.broadcasted_iota(jnp.int32, (seq, WIDE), 0)
    part = HALF // out_ref.shape[0]
    for l in range(layers):
        halves = [None, None]
        for k in range(cuts):
            for side in range(2):
                for copy in copies(l, side, k):
                    copy.wait()
            span = slice(k * depth, (k + 1) * depth)
            for side in range(2):
                _, big, _, weight = sides[side]
                term = jnp.concatenate([dot(big[l, r, :, span], weight[l, :, span]) for r in range(rolls)], axis=0)
                halves[side] = term if k == 0 else halves[side] + term
        both = jnp.concatenate(halves, axis=1)
        grams = []
        count = jnp.int32(0)
        for r in range(rolls):
            live = length_ref[r] - start_ref[0]
            c = both[r * seq : (r + 1) * seq] * (position < live).astype(f32)
            grams.append(
                lax.dot_general(c.T, c, NN, precision=lax.Precision.HIGHEST, preferred_element_type=f32)
            )
            count += jnp.clip(live, 0, seq)
        pair = jnp.where(lane < HALF, grams[0][HALF:], pltpu.roll(grams[1][HALF:], HALF, 1))
        total = grams[0] + grams[1]
        moments = jnp.where(lane < HALF, total[:HALF], total[HALF:])
        moments = jnp.where((row == 0) & (lane == 1), count.astype(f32), moments)
        for y in range(out_ref.shape[0]):
            out_ref[y, l, 0:part] = pair[y * part : (y + 1) * part]
            out_ref[y, l, part : 2 * part] = moments[y * part : (y + 1) * part]


def project(lengths, start, activations, out_grads, input_proj, output_proj, parts):
    layers, rolls, seq, width = activations.shape
    rank = input_proj.shape[1]
    cuts = 4
    part = HALF // parts
    anywhere = pl.BlockSpec(memory_space=pl.ANY)
    return pl.pallas_call(
        project_kernel,
        in_specs=[pl.BlockSpec(memory_space=pltpu.SMEM)] * 2 + [anywhere] * 4,
        out_specs=pl.BlockSpec(memory_space=pltpu.VMEM),
        out_shape=jax.ShapeDtypeStruct((parts, layers, 2 * part, WIDE), f32),
        scratch_shapes=[
            pltpu.VMEM(activations.shape, activations.dtype),
            pltpu.VMEM(out_grads.shape, out_grads.dtype),
            pltpu.VMEM(input_proj.shape, input_proj.dtype),
            pltpu.VMEM(output_proj.shape, output_proj.dtype),
            pltpu.SemaphoreType.DMA((layers, 2, cuts, 2)),
        ],
        compiler_params=pltpu.CompilerParams(vmem_limit_bytes=67_043_328),
        cost_estimate=cost(4 * layers * rolls * seq * width * rank, 4 * layers * rolls * seq * width),
        name="project",
    )(lengths, start, activations, out_grads, input_proj, output_proj)


def pack_kernel(layer_ref, keep_top, keep_low, send_top, send_low, keep_ref, send_ref):
    for k in range(keep_ref.shape[0]):
        keep_ref[k] = jnp.concatenate([keep_top[:, 0, k, :], keep_low[:, 0, k, :]], axis=1)
        send_ref[k] = jnp.concatenate([send_top[:, 0, k, :], send_low[:, 0, k, :]], axis=1)


def pack(layer, stored):
    train, _, rank, _ = stored.shape
    chunk = 8
    steps = rank // 2 // chunk

    def spec(other, low):
        def at(i, layer):
            l = 1 - layer[0] if other else layer[0]
            return (0, l, i + (steps if low else 0), 0)

        return pl.BlockSpec((train, 1, chunk, rank), at)

    out = pl.BlockSpec((chunk, train, WIDE), lambda i, layer: (i, 0, 0))
    shape = jax.ShapeDtypeStruct((rank // 2, train, WIDE), f32)
    return pl.pallas_call(
        pack_kernel,
        grid_spec=pltpu.PrefetchScalarGridSpec(
            num_scalar_prefetch=1,
            grid=(steps,),
            in_specs=[spec(False, False), spec(False, True), spec(True, False), spec(True, True)],
            out_specs=[out, out],
        ),
        out_shape=[shape, shape],
        compiler_params=pltpu.CompilerParams(vmem_limit_bytes=12 * 2**20),
        cost_estimate=cost(10_000_000, 6 * 2**20),
        name="pack",
    )(layer, stored, stored, stored, stored)


def inverse_of_pair(a):
    step = 8
    lane = lanes_of((step, WIDE))
    sub = lax.broadcasted_iota(jnp.int32, (step, WIDE), 0)
    base = jnp.where(lane < HALF, 0, HALF)
    rows = [a[i * step : (i + 1) * step] for i in range(HALF // step)]

    def spread(x, m):
        return jnp.broadcast_to(x[m : m + 1], (step, WIDE))

    for block in range(HALF // step):
        first = block * step
        columns = [
            [jnp.take_along_axis(r, base + (first + j), axis=1) for j in range(step)] for r in rows
        ]
        inside = (lane - base >= first) & (lane - base < first + step)
        identity = jnp.where(lane - base == first + sub, 1.0, 0.0)
        panel = jnp.where(inside, identity, rows[block])
        diag = list(columns[block])
        for m in range(step):
            inverse = 1.0 / spread(diag[m], m)
            is_row = sub == m
            keep = jnp.where(is_row, 0.0, diag[m])
            for j in range(m + 1, step):
                scaled = spread(diag[j], m) * inverse
                diag[j] = jnp.where(is_row, scaled, diag[j] - keep * scaled)
            scaled = spread(panel, m) * inverse
            panel = jnp.where(is_row, scaled, panel - keep * scaled)
        spreads = [spread(panel, j) for j in range(step)]
        for i in range(HALF // step):
            if i == block:
                rows[i] = panel
                continue
            taken = [c * p for c, p in zip(columns[i], spreads)]
            while len(taken) > 1:
                taken = [x + y for x, y in zip(taken[::2], taken[1::2])]
            rows[i] = jnp.where(inside, 0.0, rows[i]) - taken[0]
    return jnp.concatenate(rows, axis=0)


def score_kernel(core_ref, got_ref, own, over, out_ref, rolled):
    parts = got_ref.shape[0] // 2
    part = HALF // parts
    blocks = 2 * (got_ref.shape[1] // part - 1)
    lane = lanes_of((HALF, WIDE))
    row = lax.broadcasted_iota(jnp.int32, (HALF, WIDE), 0)
    left = lane < HALF
    at = got_ref.shape[1] - part
    moments = jnp.concatenate([got_ref[2 * y, at:] + got_ref[2 * y + 1, at:] for y in range(parts)], axis=0)
    count = jnp.broadcast_to(moments[0:1, 1:2], (HALF, WIDE))
    moments = jnp.where((row == 0) & (lane == 1), jnp.broadcast_to(moments[1:2, 0:1], (HALF, WIDE)), moments)
    mean = moments / count
    diagonal = jnp.where((lane == row) | (lane == row + HALF), mean, 0.0)
    trace_in = jnp.sum(jnp.where(left, diagonal, 0.0))
    trace_out = jnp.sum(jnp.where(left, 0.0, diagonal))
    extra = jnp.where(left, trace_in, trace_out) * (damping / HALF)
    damped = mean + jnp.where((lane == row) | (lane == row + HALF), extra, 0.0)
    factors = inverse_of_pair(damped)
    top = jnp.where(left, factors, 0.0)
    right = jnp.concatenate([top, pltpu.roll(top, HALF, 1)], axis=0)
    empty = jnp.zeros_like(right)
    right = in_two(
        jnp.concatenate(
            [jnp.concatenate([right, empty], axis=1), jnp.concatenate([empty, right], axis=1)], axis=0
        )
    )
    outer = in_two(factors[:, HALF:])
    half_lane = lanes_of((HALF // 2, WIDE)) < HALF

    def block_of(i):
        z, x, core = i // 4, i // 2 % 2, i % 2
        at = (2 * z + core) * part
        return [got_ref[2 * y + x, at : at + part] for y in range(parts)]

    group = 16
    apart = HALF // 2 + 1
    for b in range(0, blocks, group):
        g = [
            jnp.concatenate(block_of(i), axis=0)
            for i in range(b, b + group)
        ]
        g = jnp.concatenate([jnp.concatenate(g[i : i + 2], axis=1) for i in range(0, group, 2)], axis=0)
        inner = three_pass(in_two(g), right, NN)
        inner = jnp.concatenate([inner[HALF * i : HALF * (i + 1)] for i in range(group // 2)], axis=1)
        done = three_pass(outer, in_two(inner), NN)
        for i in range(group):
            up = done[: HALF // 2, WIDE * i : WIDE * (i + 1)]
            low = done[HALF // 2 :, WIDE * i : WIDE * (i + 1)]
            at = 2 * (b + i)
            rolled[pl.ds(at * apart, HALF // 2)] = jnp.where(half_lane, up, pltpu.roll(low, HALF, 1))
            rolled[pl.ds((at + 1) * apart, HALF // 2)] = jnp.where(half_lane, pltpu.roll(up, HALF, 1), low)
    scores = jnp.zeros((2 * blocks, 2 * HALF), f32)
    deep = 8
    for k in range(0, HALF // 2, deep):
        first = jnp.concatenate([rolled[pl.ds(k + i, 2 * blocks, apart)] for i in range(deep)], axis=1)
        second = jnp.concatenate([jnp.concatenate([own[k + i], over[k + i]], axis=0) for i in range(deep)], axis=1)
        scores += three_pass(in_two(first), in_two(second), NT)
    scores *= 1.0 / math.sqrt(2 * HALF * HALF)
    out_ref[...] = jnp.where(core_ref[0] == 0, scores, pltpu.roll(scores, HALF, 1))


def score(place, got, own, over):
    blocks = 2 * (got.shape[1] // (2 * HALF // got.shape[0]) - 1)
    vmem = pl.BlockSpec(memory_space=pltpu.VMEM)
    return pl.pallas_call(
        score_kernel,
        in_specs=[pl.BlockSpec(memory_space=pltpu.SMEM)] + [vmem] * 3,
        out_specs=vmem,
        out_shape=jax.ShapeDtypeStruct((2 * blocks, WIDE), f32),
        scratch_shapes=[
            pltpu.VMEM((2 * blocks * (HALF // 2 + 1), WIDE), f32),
        ],
        compiler_params=pltpu.CompilerParams(vmem_limit_bytes=16 * 2**20),
        cost_estimate=cost(200_000_000, 6 * 2**20),
        name="score",
    )(place, got, own, over)


def shards(activations, out_grads, lengths, input_proj, output_proj, stored_proj):
    seq_count = lax.axis_size(SEQ)
    core = lax.axis_index("core")
    seq_dev = activations.shape[2]
    start = (lax.axis_index(SEQ) * seq_dev).astype(jnp.int32).reshape(1)
    place = core.astype(jnp.int32).reshape(1)
    terms = project(lengths, start, activations, out_grads, input_proj, output_proj, seq_count)
    part = terms.shape[2] // 2
    terms = terms.reshape(-1, 2 * part, WIDE)
    arrived = lax.all_to_all(terms, SEQ + ("core",), 0, 0, tiled=True)
    seq_sum = arrived.reshape(seq_count, 2, 2 * part, WIDE).sum(axis=0)
    moments = seq_sum[:, part:].sum(axis=0)
    rows = jnp.concatenate([seq_sum[:, :part].reshape(-1, WIDE), moments], axis=0)
    z_count = lax.axis_size("z")
    z_all = lax.all_to_all(jnp.broadcast_to(rows, (z_count, *rows.shape)), "z", 0, 0, tiled=True)
    moments = z_all[:, 2 * part :].sum(axis=0)
    rows = jnp.concatenate([z_all[:, : 2 * part].reshape(-1, WIDE), moments], axis=0)
    rest = SEQ + ("x_hi",)
    got = lax.all_to_all(jnp.broadcast_to(rows, (lax.axis_size(rest), *rows.shape)), rest, 0, 0, tiled=True)
    own, send = pack(place, stored_proj)
    over = lax.ppermute(send, "core", [(0, 1), (1, 0)])
    partial = score(place, got, own, over)
    back = lax.all_to_all(partial.reshape(-1, 2, WIDE), BLK, 0, 0, tiled=True)
    back = back.reshape(-1, 2, 2, WIDE).sum(axis=1)
    return jnp.swapaxes(back, 0, 1).reshape(2, -1)


def solution(mesh):
    seq, blk = mesh.shape["seq"], mesh.shape["blk"]
    fine = Mesh(mesh.devices.reshape(seq // 2, 2, blk // 4, 2, 2), SEQ + BLK)
    return jax.shard_map(
        shards,
        mesh=fine,
        in_specs=(
            P(None, BLK, SEQ, None),
            P(None, BLK, SEQ, None),
            P(BLK),
            P(),
            P(),
            P(SEQ + BLK, None, None, None),
        ),
        out_specs=P(BLK, SEQ),
        check_vma=False,
    )
```

profile of v0, /device:TPU:1, one launch (start us, length us, event | category | flops | bytes accessed | tf_op | source)
XLA Modules:
  0.0 84.9 jit_solution(1999304824764717794)
XLA Ops:
  0.0 7.4 %project.1 = f32[8,2,16,128]{3,2,1,0:T(8,128)} custom-call(s32[2]{0:T(128)} %length_ref.1, s32[1]{0:T(128)} %bitcast.1.start_ref, bf16[2,2,128,4096]{3,2,1,0:T(8,128)(2,1)} %act_hbm.1, bf16[2,2,128,4096]{3,2,1,0:T(8,128)(2,1)} %grad_hbm.1, bf16[2,64,4096]{2,1,0:T(8,128)(2,1)} %win_hbm.1, bf16[2,64,4096]{2,1,0:T(8,128)(2,1)} %wout_hbm.1), custom_call_target="tpu_custom_call" | custom-call | flops 536870912 | bytes 8388608 | tf_op jit(solution)/shard_map/project/pallas_call | solution.py:104
  7.4 13.0 %all_to_all.20 = f32[16,16,128]{2,1,0:T(8,128)S(1)} all-to-all(f32[16,16,128]{2,1,0:T(8,128)} %bitcast.14), channel_id=1, replica_groups=mesh['y'=4,'x_lo'=2,'z'=8,'x_hi'=2,'core'=2] {'y','x_lo','core'}, dimensions={0} | all-to-all | bytes 262144 | tf_op jit(solution)/shard_map/all_to_all | solution.py:284
  20.5 0.6 broadcast_in_dim.6
  21.1 8.2 %all-to-all-start.1 = ((f32[8,24,128]{2,1,0:T(8,128)}), f32[8,24,128]{2,1,0:T(8,128)S(1)}, u32[]{:S(2)}, u32[]{:S(2)}) async-start(f32[8,24,128]{2,1,0:T(8,128)} %broadcast_in_dim.6), calls=%async_computation.1 | async-start | bytes 196608 | tf_op jit(solution)/shard_map/all_to_all | solution.py:289
  29.3 0.0 copy-start
  29.3 2.2 %copy-done = f32[64,2,64,64]{3,2,1,0:T(8,128)S(1)} copy-done((f32[64,2,64,64]{3,2,1,0:T(8,128)S(1)}, f32[64,2,64,64]{3,2,1,0:T(8,128)}, u32[]{:S(2)}) %copy-start) | copy-done | bytes 2097176
  31.5 3.7 %pack.1 = (f32[32,64,128]{2,1,0:T(8,128)S(1)}, f32[32,64,128]{2,1,0:T(8,128)}) custom-call(s32[1]{0:T(128)} %bitcast.layer_ref.core_ref, f32[64,2,64,64]{3,2,1,0:T(8,128)S(1)} %copy-done, f32[64,2,64,64]{3,2,1,0:T(8,128)S(1)} %copy-done, f32[64,2,64,64]{3,2,1,0:T(8,128)S(1)} %copy-done, f32[64,2,64,64]{3,2,1,0:T(8,128)S(1)} %copy-done), custom_call_target="tpu_custom_call" | custom-call | flops 10000000 | bytes 6291456 | tf_op jit(solution)/shard_map/pack/pallas_call | solution.py:142
  35.2 0.9 %collective-permute-start = (f32[32,64,128]{2,1,0:T(8,128)}, f32[32,64,128]{2,1,0:T(8,128)S(1)}, u32[]{:S(2)}, u32[]{:S(2)}) collective-permute-start(f32[32,64,128]{2,1,0:T(8,128)} %get-tuple-element.8), channel_id=1, source_target_pairs={{0,1},{1,0},{2,3},{3,2},{4,5},{5,4},{6,7},{7,6},{8,9},{9,8},{10,11... | collective-permute-start | bytes 3145736 | tf_op jit(solution)/shard_map/ppermute | solution.py:295
  36.1 0.8 all-to-all-done.1
  36.9 1.1 %broadcast_in_dim.7 = f32[16,136,128]{2,1,0:T(8,128)} broadcast(f32[136,128]{1,0:T(8,128)S(1)} %pad_maximum_fusion), dimensions={1,2} | broadcast | bytes 1183744 | tf_op jit(solution)/shard_map/broadcast_in_dim | solution.py:293
  38.0 4.3 %all-to-all-start.2 = ((f32[16,136,128]{2,1,0:T(8,128)}), f32[16,136,128]{2,1,0:T(8,128)S(1)}, u32[]{:S(2)}, u32[]{:S(2)}) async-start(f32[16,136,128]{2,1,0:T(8,128)} %broadcast_in_dim.7), calls=%async_computation.2 | async-start | bytes 2228224 | tf_op jit(solution)/shard_map/all_to_all | solution.py:293
  42.3 0.0 collective-permute-done.over
  42.3 14.2 %all-to-all-done.2.got_ref = f32[16,136,128]{2,1,0:T(8,128)S(1)} async-done(((f32[16,136,128]{2,1,0:T(8,128)}), f32[16,136,128]{2,1,0:T(8,128)S(1)}, u32[]{:S(2)}, u32[]{:S(2)}) %all-to-all-start.2) | async-done | bytes 1114144 | tf_op jit(solution)/shard_map/all_to_all | solution.py:293
  56.5 5.7 %score.1 = f32[64,128]{1,0:T(8,128)S(1)} custom-call(s32[1]{0:T(128)} %bitcast.layer_ref.core_ref, f32[16,136,128]{2,1,0:T(8,128)S(1)} %all-to-all-done.2.got_ref, f32[32,64,128]{2,1,0:T(8,128)S(1)} %get-tuple-element.7.own, f32[32,64,128]{2,1,0:T(8,128)S(1)} %collective-permute-done.over), custom_call_target="tpu_custom_call" | custom-call | flops 200000000 | bytes 6291456 | tf_op jit(solution)/shard_map/score/pallas_call | solution.py:261
  62.3 22.0 %all_to_all.21 = f32[32,2,128]{2,1,0:T(2,128)S(1)} all-to-all(f32[32,2,128]{2,1,0:T(2,128)S(1)} %bitcast.13), channel_id=1, replica_groups=mesh['y'=4,'x_lo'=2,'z'=8,'x_hi'=2,'core'=2] {'z','x_hi','core'}, dimensions={0} | all-to-all | bytes 65536 | tf_op jit(solution)/shard_map/all_to_all | solution.py:297
  84.3 0.6 bitcast_reduce_fusion
  (6 shorter events, 0.0 us)
Async XLA Ops:
  21.1 15.8 %all-to-all-start.1 = ((f32[8,24,128]{2,1,0:T(8,128)}), f32[8,24,128]{2,1,0:T(8,128)S(1)}, u32[]{:S(2)}, u32[]{:S(2)}) async-start(f32[8,24,128]{2,1,0:T(8,128)} %broadcast_in_dim.6), calls=%async_computation.1 | async-start | bytes 196608 | tf_op jit(solution)/shard_map/all_to_all | solution.py:289
  29.3 2.2 %copy-start = (f32[64,2,64,64]{3,2,1,0:T(8,128)S(1)}, f32[64,2,64,64]{3,2,1,0:T(8,128)}, u32[]{:S(2)}) copy-start(f32[64,2,64,64]{3,2,1,0:T(8,128)} %send_low.1) | copy-start | bytes 6291460
  35.2 7.2 %collective-permute-start = (f32[32,64,128]{2,1,0:T(8,128)}, f32[32,64,128]{2,1,0:T(8,128)S(1)}, u32[]{:S(2)}, u32[]{:S(2)}) collective-permute-start(f32[32,64,128]{2,1,0:T(8,128)} %get-tuple-element.8), channel_id=1, source_target_pairs={{0,1},{1,0},{2,3},{3,2},{4,5},{5,4},{6,7},{7,6},{8,9},{9,8},{10,11... | collective-permute-start | bytes 3145736 | tf_op jit(solution)/shard_map/ppermute | solution.py:295
  38.0 18.5 %all-to-all-start.2 = ((f32[16,136,128]{2,1,0:T(8,128)}), f32[16,136,128]{2,1,0:T(8,128)S(1)}, u32[]{:S(2)}, u32[]{:S(2)}) async-start(f32[16,136,128]{2,1,0:T(8,128)} %broadcast_in_dim.7), calls=%async_computation.2 | async-start | bytes 2228224 | tf_op jit(solution)/shard_map/all_to_all | solution.py:293
where the time goes:
time: 85.3 us; the launch traced here: 84.9 us
  blocking collectives  35 us (41%)
  Pallas kernels  16.8 us (20%)
  waiting for transfers between devices  15 us (18%)
  starting transfers between devices  13.4 us (16%)
  local copies, waits for them, and re-layouts  3.88 us (5%)
    all_to_all x1, blocking collectives, shards(): back = lax.all_to_all(partial.reshape(-1, 2, WIDE), BLK, 0, 0, tiled=True)  22 us
    all_to_all x1, waiting for transfers between devices, shards(): lax.all_to_all(jnp.broadcast_to(rows, (lax.axis_size(rest), *rows.shape))...  14.2 us
    all_to_all x1, blocking collectives, shards(): arrived = lax.all_to_all(terms, SEQ + ('core',), 0, 0, tiled=True)  13 us
    all_to_all x1, starting transfers between devices, shards(): lax.all_to_all(jnp.broadcast_to(rows, (z_count, *rows.shape)), 'z', 0, 0,...  8.18 us
    pallas_call x1, Pallas kernels, project(): pl.pallas_call(project_kernel, in_specs=[pl.BlockSpec(memory_space=pltpu....  7.42 us
    pallas_call x1, Pallas kernels, score(): pl.pallas_call(score_kernel, in_specs=[pl.BlockSpec(memory_space=pltpu.SM...  5.74 us
    all_to_all x1, starting transfers between devices, shards(): lax.all_to_all(jnp.broadcast_to(rows, (lax.axis_size(rest), *rows.shape))...  4.32 us
    pallas_call x1, Pallas kernels, pack(): pl.pallas_call(pack_kernel, grid_spec=pltpu.PrefetchScalarGridSpec(num_sc...  3.66 us
  transfers between devices with their start and end apart: 3, of which 2 were waited for; matrix products, arithmetic and copies ran while one was open for 1% of the time, Pallas kernels for 4%

commit v1 on v0

--- a/solution.py
+++ b/solution.py
@@ -40,7 +40,7 @@
     return stacked[:rows] + (stacked[rows:] + dot(a[0], b[1]))
 
 
-def project_kernel(length_ref, start_ref, act_hbm, grad_hbm, win_hbm, wout_hbm, out_ref, act, grad, win, wout, sems):
+def project_kernel(length_ref, start_ref, place_ref, act_hbm, grad_hbm, win_hbm, wout_hbm, out_ref, act, grad, win, wout, sems):
     layers, rolls, seq, width = act.shape
     cuts = sems.shape[2]
     depth = width // cuts
@@ -95,7 +95,7 @@
             out_ref[y, l, part : 2 * part] = moments[y * part : (y + 1) * part]
 
 
-def project(lengths, start, activations, out_grads, input_proj, output_proj, parts):
+def project(lengths, start, place, activations, out_grads, input_proj, output_proj, parts):
     layers, rolls, seq, width = activations.shape
     rank = input_proj.shape[1]
     cuts = 4
@@ -103,7 +103,7 @@
     anywhere = pl.BlockSpec(memory_space=pl.ANY)
     return pl.pallas_call(
         project_kernel,
-        in_specs=[pl.BlockSpec(memory_space=pltpu.SMEM)] * 2 + [anywhere] * 4,
+        in_specs=[pl.BlockSpec(memory_space=pltpu.SMEM)] * 3 + [anywhere] * 4,
         out_specs=pl.BlockSpec(memory_space=pltpu.VMEM),
         out_shape=jax.ShapeDtypeStruct((parts, layers, 2 * part, WIDE), f32),
         scratch_shapes=[
@@ -113,10 +113,10 @@
             pltpu.VMEM(output_proj.shape, output_proj.dtype),
             pltpu.SemaphoreType.DMA((layers, 2, cuts, 2)),
         ],
-        compiler_params=pltpu.CompilerParams(vmem_limit_bytes=67_043_328),
+        compiler_params=pltpu.CompilerParams(vmem_limit_bytes=65_700_000),
         cost_estimate=cost(4 * layers * rolls * seq * width * rank, 4 * layers * rolls * seq * width),
         name="project",
-    )(lengths, start, activations, out_grads, input_proj, output_proj)
+    )(lengths, start, place, activations, out_grads, input_proj, output_proj)
 
 
 def pack_kernel(layer_ref, keep_top, keep_low, send_top, send_low, keep_ref, send_ref):
@@ -278,7 +278,7 @@
     seq_dev = activations.shape[2]
     start = (lax.axis_index(SEQ) * seq_dev).astype(jnp.int32).reshape(1)
     place = core.astype(jnp.int32).reshape(1)
-    terms = project(lengths, start, activations, out_grads, input_proj, output_proj, seq_count)
+    terms = project(lengths, start, place, activations, out_grads, input_proj, output_proj, seq_count)
     part = terms.shape[2] // 2
     terms = terms.reshape(-1, 2 * part, WIDE)
     arrived = lax.all_to_all(terms, SEQ + ("core",), 0, 0, tiled=True)

time: 85.3 us -> 85.3 us (level)
  no operation moved by 1% of the time
where the time goes in v1:
time: 85.3 us; the launch traced here: 84.9 us
  blocking collectives  35 us (41%)
  Pallas kernels  16.8 us (20%)
  waiting for transfers between devices  15 us (18%)
  starting transfers between devices  13.4 us (16%)
  local copies, waits for them, and re-layouts  3.88 us (5%)
    all_to_all x1, blocking collectives, shards(): back = lax.all_to_all(partial.reshape(-1, 2, WIDE), BLK, 0, 0, tiled=True)  22 us
    all_to_all x1, waiting for transfers between devices, shards(): lax.all_to_all(jnp.broadcast_to(rows, (lax.axis_size(rest), *rows.shape))...  14.2 us
    all_to_all x1, blocking collectives, shards(): arrived = lax.all_to_all(terms, SEQ + ('core',), 0, 0, tiled=True)  13 us
    all_to_all x1, starting transfers between devices, shards(): lax.all_to_all(jnp.broadcast_to(rows, (z_count, *rows.shape)), 'z', 0, 0,...  8.18 us
    pallas_call x1, Pallas kernels, project(): pl.pallas_call(project_kernel, in_specs=[pl.BlockSpec(memory_space=pltpu....  7.42 us
    pallas_call x1, Pallas kernels, score(): pl.pallas_call(score_kernel, in_specs=[pl.BlockSpec(memory_space=pltpu.SM...  5.74 us
    all_to_all x1, starting transfers between devices, shards(): lax.all_to_all(jnp.broadcast_to(rows, (lax.axis_size(rest), *rows.shape))...  4.32 us
    pallas_call x1, Pallas kernels, pack(): pl.pallas_call(pack_kernel, grid_spec=pltpu.PrefetchScalarGridSpec(num_sc...  3.66 us
  transfers between devices with their start and end apart: 3, of which 2 were waited for; matrix products, arithmetic and copies ran while one was open for 1% of the time, Pallas kernels for 4%

profile of v1, /device:TPU:1, one launch (start us, length us, event | category | flops | bytes accessed | tf_op | source)
XLA Modules:
  0.0 84.9 jit_solution(16501898447860891299)
XLA Ops:
  0.0 7.4 %project.1 = f32[8,2,16,128]{3,2,1,0:T(8,128)} custom-call(s32[2]{0:T(128)} %length_ref.1, s32[1]{0:T(128)} %bitcast.1.start_ref, s32[1]{0:T(128)} %bitcast.place_ref.layer_ref.core_ref, bf16[2,2,128,4096]{3,2,1,0:T(8,128)(2,1)} %act_hbm.1, bf16[2,2,128,4096]{3,2,1,0:T(8,128)(2,1)} %grad_hbm.1, bf16[2,64,4096]{2,1,0:T(8,128)(2,1)} %win_hbm.1, ...), custom_call_target="tpu_custom_call" | custom-call | flops 536870912 | bytes 8388608 | tf_op jit(solution)/shard_map/project/pallas_call | solution.py:104
  7.4 13.0 %all_to_all.20 = f32[16,16,128]{2,1,0:T(8,128)S(1)} all-to-all(f32[16,16,128]{2,1,0:T(8,128)} %bitcast.14), channel_id=1, replica_groups=mesh['y'=4,'x_lo'=2,'z'=8,'x_hi'=2,'core'=2] {'y','x_lo','core'}, dimensions={0} | all-to-all | bytes 262144 | tf_op jit(solution)/shard_map/all_to_all | solution.py:284
  20.5 0.6 broadcast_in_dim.6
  21.1 8.2 %all-to-all-start.1 = ((f32[8,24,128]{2,1,0:T(8,128)}), f32[8,24,128]{2,1,0:T(8,128)S(1)}, u32[]{:S(2)}, u32[]{:S(2)}) async-start(f32[8,24,128]{2,1,0:T(8,128)} %broadcast_in_dim.6), calls=%async_computation.1 | async-start | bytes 196608 | tf_op jit(solution)/shard_map/all_to_all | solution.py:289
  29.3 0.0 copy-start
  29.3 2.2 %copy-done = f32[64,2,64,64]{3,2,1,0:T(8,128)S(1)} copy-done((f32[64,2,64,64]{3,2,1,0:T(8,128)S(1)}, f32[64,2,64,64]{3,2,1,0:T(8,128)}, u32[]{:S(2)}) %copy-start) | copy-done | bytes 2097176
  31.5 3.7 %pack.1 = (f32[32,64,128]{2,1,0:T(8,128)S(1)}, f32[32,64,128]{2,1,0:T(8,128)}) custom-call(s32[1]{0:T(128)} %bitcast.place_ref.layer_ref.core_ref, f32[64,2,64,64]{3,2,1,0:T(8,128)S(1)} %copy-done, f32[64,2,64,64]{3,2,1,0:T(8,128)S(1)} %copy-done, f32[64,2,64,64]{3,2,1,0:T(8,128)S(1)} %copy-done, f32[64,2,64,64]{3,2,1,0:T(8,128)S(1)} %copy-done), custom_call_target="tpu_custom_call" | custom-call | flops 10000000 | bytes 6291456 | tf_op jit(solution)/shard_map/pack/pallas_call | solution.py:142
  35.2 0.9 %collective-permute-start = (f32[32,64,128]{2,1,0:T(8,128)}, f32[32,64,128]{2,1,0:T(8,128)S(1)}, u32[]{:S(2)}, u32[]{:S(2)}) collective-permute-start(f32[32,64,128]{2,1,0:T(8,128)} %get-tuple-element.8), channel_id=1, source_target_pairs={{0,1},{1,0},{2,3},{3,2},{4,5},{5,4},{6,7},{7,6},{8,9},{9,8},{10,11... | collective-permute-start | bytes 3145736 | tf_op jit(solution)/shard_map/ppermute | solution.py:295
  36.1 0.8 all-to-all-done.1
  36.9 1.1 %broadcast_in_dim.7 = f32[16,136,128]{2,1,0:T(8,128)} broadcast(f32[136,128]{1,0:T(8,128)S(1)} %pad_maximum_fusion), dimensions={1,2} | broadcast | bytes 1183744 | tf_op jit(solution)/shard_map/broadcast_in_dim | solution.py:293
  38.0 4.3 %all-to-all-start.2 = ((f32[16,136,128]{2,1,0:T(8,128)}), f32[16,136,128]{2,1,0:T(8,128)S(1)}, u32[]{:S(2)}, u32[]{:S(2)}) async-start(f32[16,136,128]{2,1,0:T(8,128)} %broadcast_in_dim.7), calls=%async_computation.2 | async-start | bytes 2228224 | tf_op jit(solution)/shard_map/all_to_all | solution.py:293
  42.3 0.0 collective-permute-done.over
  42.3 14.2 %all-to-all-done.2.got_ref = f32[16,136,128]{2,1,0:T(8,128)S(1)} async-done(((f32[16,136,128]{2,1,0:T(8,128)}), f32[16,136,128]{2,1,0:T(8,128)S(1)}, u32[]{:S(2)}, u32[]{:S(2)}) %all-to-all-start.2) | async-done | bytes 1114144 | tf_op jit(solution)/shard_map/all_to_all | solution.py:293
  56.5 5.7 %score.1 = f32[64,128]{1,0:T(8,128)S(1)} custom-call(s32[1]{0:T(128)} %bitcast.place_ref.layer_ref.core_ref, f32[16,136,128]{2,1,0:T(8,128)S(1)} %all-to-all-done.2.got_ref, f32[32,64,128]{2,1,0:T(8,128)S(1)} %get-tuple-element.7.own, f32[32,64,128]{2,1,0:T(8,128)S(1)} %collective-permute-done.over), custom_call_target="tpu_custom_call" | custom-call | flops 200000000 | bytes 6291456 | tf_op jit(solution)/shard_map/score/pallas_call | solution.py:261
  62.3 22.0 %all_to_all.21 = f32[32,2,128]{2,1,0:T(2,128)S(1)} all-to-all(f32[32,2,128]{2,1,0:T(2,128)S(1)} %bitcast.13), channel_id=1, replica_groups=mesh['y'=4,'x_lo'=2,'z'=8,'x_hi'=2,'core'=2] {'z','x_hi','core'}, dimensions={0} | all-to-all | bytes 65536 | tf_op jit(solution)/shard_map/all_to_all | solution.py:297
  84.3 0.6 bitcast_reduce_fusion
  (6 shorter events, 0.0 us)
Async XLA Ops:
  21.1 15.8 %all-to-all-start.1 = ((f32[8,24,128]{2,1,0:T(8,128)}), f32[8,24,128]{2,1,0:T(8,128)S(1)}, u32[]{:S(2)}, u32[]{:S(2)}) async-start(f32[8,24,128]{2,1,0:T(8,128)} %broadcast_in_dim.6), calls=%async_computation.1 | async-start | bytes 196608 | tf_op jit(solution)/shard_map/all_to_all | solution.py:289
  29.3 2.2 %copy-start = (f32[64,2,64,64]{3,2,1,0:T(8,128)S(1)}, f32[64,2,64,64]{3,2,1,0:T(8,128)}, u32[]{:S(2)}) copy-start(f32[64,2,64,64]{3,2,1,0:T(8,128)} %send_low.1) | copy-start | bytes 6291460
  35.2 7.2 %collective-permute-start = (f32[32,64,128]{2,1,0:T(8,128)}, f32[32,64,128]{2,1,0:T(8,128)S(1)}, u32[]{:S(2)}, u32[]{:S(2)}) collective-permute-start(f32[32,64,128]{2,1,0:T(8,128)} %get-tuple-element.8), channel_id=1, source_target_pairs={{0,1},{1,0},{2,3},{3,2},{4,5},{5,4},{6,7},{7,6},{8,9},{9,8},{10,11... | collective-permute-start | bytes 3145736 | tf_op jit(solution)/shard_map/ppermute | solution.py:295
  38.0 18.5 %all-to-all-start.2 = ((f32[16,136,128]{2,1,0:T(8,128)}), f32[16,136,128]{2,1,0:T(8,128)S(1)}, u32[]{:S(2)}, u32[]{:S(2)}) async-start(f32[16,136,128]{2,1,0:T(8,128)} %broadcast_in_dim.7), calls=%async_computation.2 | async-start | bytes 2228224 | tf_op jit(solution)/shard_map/all_to_all | solution.py:293

commit v2 on v1

--- a/solution.py
+++ b/solution.py
@@ -178,10 +178,10 @@
             is_row = sub == m
             keep = jnp.where(is_row, 0.0, diag[m])
             for j in range(m + 1, step):
-                scaled = spread(diag[j], m) * inverse
-                diag[j] = jnp.where(is_row, scaled, diag[j] - keep * scaled)
-            scaled = spread(panel, m) * inverse
-            panel = jnp.where(is_row, scaled, panel - keep * scaled)
+                over = spread(diag[j], m)
+                diag[j] = jnp.where(is_row, 0.0, diag[j]) + jnp.where(is_row, over, -(keep * over)) * inverse
+            over = spread(panel, m)
+            panel = jnp.where(is_row, 0.0, panel) + jnp.where(is_row, over, -(keep * over)) * inverse
         spreads = [spread(panel, j) for j in range(step)]
         for i in range(HALF // step):
             if i == block:

time: 85.3 us -> 84.8 us (level)
  no operation moved by 1% of the time
where the time goes in v2:
time: 84.8 us; the launch traced here: 84.4 us
  blocking collectives  35 us (41%)
  Pallas kernels  16.4 us (19%)
  waiting for transfers between devices  15 us (18%)
  starting transfers between devices  13.4 us (16%)
  local copies, waits for them, and re-layouts  3.88 us (5%)
    all_to_all x1, blocking collectives, shards(): back = lax.all_to_all(partial.reshape(-1, 2, WIDE), BLK, 0, 0, tiled=True)  22 us
    all_to_all x1, waiting for transfers between devices, shards(): lax.all_to_all(jnp.broadcast_to(rows, (lax.axis_size(rest), *rows.shape))...  14.2 us
    all_to_all x1, blocking collectives, shards(): arrived = lax.all_to_all(terms, SEQ + ('core',), 0, 0, tiled=True)  13 us
    all_to_all x1, starting transfers between devices, shards(): lax.all_to_all(jnp.broadcast_to(rows, (z_count, *rows.shape)), 'z', 0, 0,...  8.18 us
    pallas_call x1, Pallas kernels, project(): pl.pallas_call(project_kernel, in_specs=[pl.BlockSpec(memory_space=pltpu....  7.42 us
    pallas_call x1, Pallas kernels, score(): pl.pallas_call(score_kernel, in_specs=[pl.BlockSpec(memory_space=pltpu.SM...  5.28 us
    all_to_all x1, starting transfers between devices, shards(): lax.all_to_all(jnp.broadcast_to(rows, (lax.axis_size(rest), *rows.shape))...  4.32 us
    pallas_call x1, Pallas kernels, pack(): pl.pallas_call(pack_kernel, grid_spec=pltpu.PrefetchScalarGridSpec(num_sc...  3.66 us
  transfers between devices with their start and end apart: 3, of which 2 were waited for; matrix products, arithmetic and copies ran while one was open for 1% of the time, Pallas kernels for 4%

profile of v2, /device:TPU:1, one launch (start us, length us, event | category | flops | bytes accessed | tf_op | source)
XLA Modules:
  0.0 84.4 jit_solution(9349819675492197357)
XLA Ops:
  0.0 7.4 %project.1 = f32[8,2,16,128]{3,2,1,0:T(8,128)} custom-call(s32[2]{0:T(128)} %length_ref.1, s32[1]{0:T(128)} %bitcast.1.start_ref, s32[1]{0:T(128)} %bitcast.place_ref.layer_ref.core_ref, bf16[2,2,128,4096]{3,2,1,0:T(8,128)(2,1)} %act_hbm.1, bf16[2,2,128,4096]{3,2,1,0:T(8,128)(2,1)} %grad_hbm.1, bf16[2,64,4096]{2,1,0:T(8,128)(2,1)} %win_hbm.1, ...), custom_call_target="tpu_custom_call" | custom-call | flops 536870912 | bytes 8388608 | tf_op jit(solution)/shard_map/project/pallas_call | solution.py:104
  7.4 13.0 %all_to_all.20 = f32[16,16,128]{2,1,0:T(8,128)S(1)} all-to-all(f32[16,16,128]{2,1,0:T(8,128)} %bitcast.14), channel_id=1, replica_groups=mesh['y'=4,'x_lo'=2,'z'=8,'x_hi'=2,'core'=2] {'y','x_lo','core'}, dimensions={0} | all-to-all | bytes 262144 | tf_op jit(solution)/shard_map/all_to_all | solution.py:284
  20.5 0.6 broadcast_in_dim.6
  21.1 8.2 %all-to-all-start.1 = ((f32[8,24,128]{2,1,0:T(8,128)}), f32[8,24,128]{2,1,0:T(8,128)S(1)}, u32[]{:S(2)}, u32[]{:S(2)}) async-start(f32[8,24,128]{2,1,0:T(8,128)} %broadcast_in_dim.6), calls=%async_computation.1 | async-start | bytes 196608 | tf_op jit(solution)/shard_map/all_to_all | solution.py:289
  29.3 0.0 copy-start
  29.3 2.2 %copy-done = f32[64,2,64,64]{3,2,1,0:T(8,128)S(1)} copy-done((f32[64,2,64,64]{3,2,1,0:T(8,128)S(1)}, f32[64,2,64,64]{3,2,1,0:T(8,128)}, u32[]{:S(2)}) %copy-start) | copy-done | bytes 2097176
  31.5 3.7 %pack.1 = (f32[32,64,128]{2,1,0:T(8,128)S(1)}, f32[32,64,128]{2,1,0:T(8,128)}) custom-call(s32[1]{0:T(128)} %bitcast.place_ref.layer_ref.core_ref, f32[64,2,64,64]{3,2,1,0:T(8,128)S(1)} %copy-done, f32[64,2,64,64]{3,2,1,0:T(8,128)S(1)} %copy-done, f32[64,2,64,64]{3,2,1,0:T(8,128)S(1)} %copy-done, f32[64,2,64,64]{3,2,1,0:T(8,128)S(1)} %copy-done), custom_call_target="tpu_custom_call" | custom-call | flops 10000000 | bytes 6291456 | tf_op jit(solution)/shard_map/pack/pallas_call | solution.py:142
  35.2 0.9 %collective-permute-start = (f32[32,64,128]{2,1,0:T(8,128)}, f32[32,64,128]{2,1,0:T(8,128)S(1)}, u32[]{:S(2)}, u32[]{:S(2)}) collective-permute-start(f32[32,64,128]{2,1,0:T(8,128)} %get-tuple-element.8), channel_id=1, source_target_pairs={{0,1},{1,0},{2,3},{3,2},{4,5},{5,4},{6,7},{7,6},{8,9},{9,8},{10,11... | collective-permute-start | bytes 3145736 | tf_op jit(solution)/shard_map/ppermute | solution.py:295
  36.1 0.8 all-to-all-done.1
  36.9 1.1 %broadcast_in_dim.7 = f32[16,136,128]{2,1,0:T(8,128)} broadcast(f32[136,128]{1,0:T(8,128)S(1)} %pad_maximum_fusion), dimensions={1,2} | broadcast | bytes 1183744 | tf_op jit(solution)/shard_map/broadcast_in_dim | solution.py:293
  38.0 4.3 %all-to-all-start.2 = ((f32[16,136,128]{2,1,0:T(8,128)}), f32[16,136,128]{2,1,0:T(8,128)S(1)}, u32[]{:S(2)}, u32[]{:S(2)}) async-start(f32[16,136,128]{2,1,0:T(8,128)} %broadcast_in_dim.7), calls=%async_computation.2 | async-start | bytes 2228224 | tf_op jit(solution)/shard_map/all_to_all | solution.py:293
  42.3 0.0 collective-permute-done.over
  42.3 14.2 %all-to-all-done.2.got_ref = f32[16,136,128]{2,1,0:T(8,128)S(1)} async-done(((f32[16,136,128]{2,1,0:T(8,128)}), f32[16,136,128]{2,1,0:T(8,128)S(1)}, u32[]{:S(2)}, u32[]{:S(2)}) %all-to-all-start.2) | async-done | bytes 1114144 | tf_op jit(solution)/shard_map/all_to_all | solution.py:293
  56.5 5.3 %score.1 = f32[64,128]{1,0:T(8,128)S(1)} custom-call(s32[1]{0:T(128)} %bitcast.place_ref.layer_ref.core_ref, f32[16,136,128]{2,1,0:T(8,128)S(1)} %all-to-all-done.2.got_ref, f32[32,64,128]{2,1,0:T(8,128)S(1)} %get-tuple-element.7.own, f32[32,64,128]{2,1,0:T(8,128)S(1)} %collective-permute-done.over), custom_call_target="tpu_custom_call" | custom-call | flops 200000000 | bytes 6291456 | tf_op jit(solution)/shard_map/score/pallas_call | solution.py:261
  61.8 22.0 %all_to_all.21 = f32[32,2,128]{2,1,0:T(2,128)S(1)} all-to-all(f32[32,2,128]{2,1,0:T(2,128)S(1)} %bitcast.13), channel_id=1, replica_groups=mesh['y'=4,'x_lo'=2,'z'=8,'x_hi'=2,'core'=2] {'z','x_hi','core'}, dimensions={0} | all-to-all | bytes 65536 | tf_op jit(solution)/shard_map/all_to_all | solution.py:297
  83.8 0.6 bitcast_reduce_fusion
  (6 shorter events, 0.0 us)
Async XLA Ops:
  21.1 15.8 %all-to-all-start.1 = ((f32[8,24,128]{2,1,0:T(8,128)}), f32[8,24,128]{2,1,0:T(8,128)S(1)}, u32[]{:S(2)}, u32[]{:S(2)}) async-start(f32[8,24,128]{2,1,0:T(8,128)} %broadcast_in_dim.6), calls=%async_computation.1 | async-start | bytes 196608 | tf_op jit(solution)/shard_map/all_to_all | solution.py:289
  29.3 2.2 %copy-start = (f32[64,2,64,64]{3,2,1,0:T(8,128)S(1)}, f32[64,2,64,64]{3,2,1,0:T(8,128)}, u32[]{:S(2)}) copy-start(f32[64,2,64,64]{3,2,1,0:T(8,128)} %send_low.1) | copy-start | bytes 6291460
  35.2 7.2 %collective-permute-start = (f32[32,64,128]{2,1,0:T(8,128)}, f32[32,64,128]{2,1,0:T(8,128)S(1)}, u32[]{:S(2)}, u32[]{:S(2)}) collective-permute-start(f32[32,64,128]{2,1,0:T(8,128)} %get-tuple-element.8), channel_id=1, source_target_pairs={{0,1},{1,0},{2,3},{3,2},{4,5},{5,4},{6,7},{7,6},{8,9},{9,8},{10,11... | collective-permute-start | bytes 3145736 | tf_op jit(solution)/shard_map/ppermute | solution.py:295
  38.0 18.5 %all-to-all-start.2 = ((f32[16,136,128]{2,1,0:T(8,128)}), f32[16,136,128]{2,1,0:T(8,128)S(1)}, u32[]{:S(2)}, u32[]{:S(2)}) async-start(f32[16,136,128]{2,1,0:T(8,128)} %broadcast_in_dim.7), calls=%async_computation.2 | async-start | bytes 2228224 | tf_op jit(solution)/shard_map/all_to_all | solution.py:293

commit v3 on v2

--- a/solution.py
+++ b/solution.py
@@ -82,9 +82,7 @@
         for r in range(rolls):
             live = length_ref[r] - start_ref[0]
             c = both[r * seq : (r + 1) * seq] * (position < live).astype(f32)
-            grams.append(
-                lax.dot_general(c.T, c, NN, precision=lax.Precision.HIGHEST, preferred_element_type=f32)
-            )
+            grams.append(three_pass(in_two(c.T), in_two(c), NN))
             count += jnp.clip(live, 0, seq)
         pair = jnp.where(lane < HALF, grams[0][HALF:], pltpu.roll(grams[1][HALF:], HALF, 1))
         total = grams[0] + grams[1]
@@ -246,7 +244,7 @@
             rolled[pl.ds(at * apart, HALF // 2)] = jnp.where(half_lane, up, pltpu.roll(low, HALF, 1))
             rolled[pl.ds((at + 1) * apart, HALF // 2)] = jnp.where(half_lane, pltpu.roll(up, HALF, 1), low)
     scores = jnp.zeros((2 * blocks, 2 * HALF), f32)
-    deep = 8
+    deep = 16
     for k in range(0, HALF // 2, deep):
         first = jnp.concatenate([rolled[pl.ds(k + i, 2 * blocks, apart)] for i in range(deep)], axis=1)
         second = jnp.concatenate([jnp.concatenate([own[k + i], over[k + i]], axis=0) for i in range(deep)], axis=1)

time: 84.8 us -> 84.1 us (level)
  no operation moved by 1% of the time
where the time goes in v3:
time: 84.1 us; the launch traced here: 83.7 us
  blocking collectives  35 us (42%)
  Pallas kernels  15.6 us (19%)
  waiting for transfers between devices  15 us (18%)
  starting transfers between devices  13.4 us (16%)
  local copies, waits for them, and re-layouts  3.88 us (5%)
    all_to_all x1, blocking collectives, shards(): back = lax.all_to_all(partial.reshape(-1, 2, WIDE), BLK, 0, 0, tiled=True)  22 us
    all_to_all x1, waiting for transfers between devices, shards(): lax.all_to_all(jnp.broadcast_to(rows, (lax.axis_size(rest), *rows.shape))...  14.2 us
    all_to_all x1, blocking collectives, shards(): arrived = lax.all_to_all(terms, SEQ + ('core',), 0, 0, tiled=True)  13 us
    all_to_all x1, starting transfers between devices, shards(): lax.all_to_all(jnp.broadcast_to(rows, (z_count, *rows.shape)), 'z', 0, 0,...  8.18 us
    pallas_call x1, Pallas kernels, project(): pl.pallas_call(project_kernel, in_specs=[pl.BlockSpec(memory_space=pltpu....  6.68 us
    pallas_call x1, Pallas kernels, score(): pl.pallas_call(score_kernel, in_specs=[pl.BlockSpec(memory_space=pltpu.SM...  5.27 us
    all_to_all x1, starting transfers between devices, shards(): lax.all_to_all(jnp.broadcast_to(rows, (lax.axis_size(rest), *rows.shape))...  4.32 us
    pallas_call x1, Pallas kernels, pack(): pl.pallas_call(pack_kernel, grid_spec=pltpu.PrefetchScalarGridSpec(num_sc...  3.66 us
  transfers between devices with their start and end apart: 3, of which 2 were waited for; matrix products, arithmetic and copies ran while one was open for 1% of the time, Pallas kernels for 4%

profile of v3, /device:TPU:1, one launch (start us, length us, event | category | flops | bytes accessed | tf_op | source)
XLA Modules:
  0.0 83.7 jit_solution(15238991568866245678)
XLA Ops:
  0.0 6.7 %project.1 = f32[8,2,16,128]{3,2,1,0:T(8,128)} custom-call(s32[2]{0:T(128)} %length_ref.1, s32[1]{0:T(128)} %bitcast.1.start_ref, s32[1]{0:T(128)} %bitcast.place_ref.layer_ref.core_ref, bf16[2,2,128,4096]{3,2,1,0:T(8,128)(2,1)} %act_hbm.1, bf16[2,2,128,4096]{3,2,1,0:T(8,128)(2,1)} %grad_hbm.1, bf16[2,64,4096]{2,1,0:T(8,128)(2,1)} %win_hbm.1, ...), custom_call_target="tpu_custom_call" | custom-call | flops 536870912 | bytes 8388608 | tf_op jit(solution)/shard_map/project/pallas_call | solution.py:102
  6.7 13.0 %all_to_all.20 = f32[16,16,128]{2,1,0:T(8,128)S(1)} all-to-all(f32[16,16,128]{2,1,0:T(8,128)} %bitcast.14), channel_id=1, replica_groups=mesh['y'=4,'x_lo'=2,'z'=8,'x_hi'=2,'core'=2] {'y','x_lo','core'}, dimensions={0} | all-to-all | bytes 262144 | tf_op jit(solution)/shard_map/all_to_all | solution.py:282
  19.8 0.6 broadcast_in_dim.6
  20.4 8.2 %all-to-all-start.1 = ((f32[8,24,128]{2,1,0:T(8,128)}), f32[8,24,128]{2,1,0:T(8,128)S(1)}, u32[]{:S(2)}, u32[]{:S(2)}) async-start(f32[8,24,128]{2,1,0:T(8,128)} %broadcast_in_dim.6), calls=%async_computation.1 | async-start | bytes 196608 | tf_op jit(solution)/shard_map/all_to_all | solution.py:287
  28.6 0.0 copy-start
  28.6 2.2 %copy-done = f32[64,2,64,64]{3,2,1,0:T(8,128)S(1)} copy-done((f32[64,2,64,64]{3,2,1,0:T(8,128)S(1)}, f32[64,2,64,64]{3,2,1,0:T(8,128)}, u32[]{:S(2)}) %copy-start) | copy-done | bytes 2097176
  30.8 3.7 %pack.1 = (f32[32,64,128]{2,1,0:T(8,128)S(1)}, f32[32,64,128]{2,1,0:T(8,128)}) custom-call(s32[1]{0:T(128)} %bitcast.place_ref.layer_ref.core_ref, f32[64,2,64,64]{3,2,1,0:T(8,128)S(1)} %copy-done, f32[64,2,64,64]{3,2,1,0:T(8,128)S(1)} %copy-done, f32[64,2,64,64]{3,2,1,0:T(8,128)S(1)} %copy-done, f32[64,2,64,64]{3,2,1,0:T(8,128)S(1)} %copy-done), custom_call_target="tpu_custom_call" | custom-call | flops 10000000 | bytes 6291456 | tf_op jit(solution)/shard_map/pack/pallas_call | solution.py:140
  34.4 0.9 %collective-permute-start = (f32[32,64,128]{2,1,0:T(8,128)}, f32[32,64,128]{2,1,0:T(8,128)S(1)}, u32[]{:S(2)}, u32[]{:S(2)}) collective-permute-start(f32[32,64,128]{2,1,0:T(8,128)} %get-tuple-element.8), channel_id=1, source_target_pairs={{0,1},{1,0},{2,3},{3,2},{4,5},{5,4},{6,7},{7,6},{8,9},{9,8},{10,11... | collective-permute-start | bytes 3145736 | tf_op jit(solution)/shard_map/ppermute | solution.py:293
  35.4 0.8 all-to-all-done.1
  36.2 1.1 %broadcast_in_dim.7 = f32[16,136,128]{2,1,0:T(8,128)} broadcast(f32[136,128]{1,0:T(8,128)S(1)} %pad_maximum_fusion), dimensions={1,2} | broadcast | bytes 1183744 | tf_op jit(solution)/shard_map/broadcast_in_dim | solution.py:291
  37.3 4.3 %all-to-all-start.2 = ((f32[16,136,128]{2,1,0:T(8,128)}), f32[16,136,128]{2,1,0:T(8,128)S(1)}, u32[]{:S(2)}, u32[]{:S(2)}) async-start(f32[16,136,128]{2,1,0:T(8,128)} %broadcast_in_dim.7), calls=%async_computation.2 | async-start | bytes 2228224 | tf_op jit(solution)/shard_map/all_to_all | solution.py:291
  41.6 0.0 collective-permute-done.over
  41.6 14.2 %all-to-all-done.2.got_ref = f32[16,136,128]{2,1,0:T(8,128)S(1)} async-done(((f32[16,136,128]{2,1,0:T(8,128)}), f32[16,136,128]{2,1,0:T(8,128)S(1)}, u32[]{:S(2)}, u32[]{:S(2)}) %all-to-all-start.2) | async-done | bytes 1114144 | tf_op jit(solution)/shard_map/all_to_all | solution.py:291
  55.8 5.3 %score.1 = f32[64,128]{1,0:T(8,128)S(1)} custom-call(s32[1]{0:T(128)} %bitcast.place_ref.layer_ref.core_ref, f32[16,136,128]{2,1,0:T(8,128)S(1)} %all-to-all-done.2.got_ref, f32[32,64,128]{2,1,0:T(8,128)S(1)} %get-tuple-element.7.own, f32[32,64,128]{2,1,0:T(8,128)S(1)} %collective-permute-done.over), custom_call_target="tpu_custom_call" | custom-call | flops 200000000 | bytes 6291456 | tf_op jit(solution)/shard_map/score/pallas_call | solution.py:259
  61.1 22.0 %all_to_all.21 = f32[32,2,128]{2,1,0:T(2,128)S(1)} all-to-all(f32[32,2,128]{2,1,0:T(2,128)S(1)} %bitcast.13), channel_id=1, replica_groups=mesh['y'=4,'x_lo'=2,'z'=8,'x_hi'=2,'core'=2] {'z','x_hi','core'}, dimensions={0} | all-to-all | bytes 65536 | tf_op jit(solution)/shard_map/all_to_all | solution.py:295
  83.0 0.6 bitcast_reduce_fusion
  (6 shorter events, 0.0 us)
Async XLA Ops:
  20.4 15.8 %all-to-all-start.1 = ((f32[8,24,128]{2,1,0:T(8,128)}), f32[8,24,128]{2,1,0:T(8,128)S(1)}, u32[]{:S(2)}, u32[]{:S(2)}) async-start(f32[8,24,128]{2,1,0:T(8,128)} %broadcast_in_dim.6), calls=%async_computation.1 | async-start | bytes 196608 | tf_op jit(solution)/shard_map/all_to_all | solution.py:287
  28.6 2.2 %copy-start = (f32[64,2,64,64]{3,2,1,0:T(8,128)S(1)}, f32[64,2,64,64]{3,2,1,0:T(8,128)}, u32[]{:S(2)}) copy-start(f32[64,2,64,64]{3,2,1,0:T(8,128)} %send_low.1) | copy-start | bytes 6291460
  34.4 7.2 %collective-permute-start = (f32[32,64,128]{2,1,0:T(8,128)}, f32[32,64,128]{2,1,0:T(8,128)S(1)}, u32[]{:S(2)}, u32[]{:S(2)}) collective-permute-start(f32[32,64,128]{2,1,0:T(8,128)} %get-tuple-element.8), channel_id=1, source_target_pairs={{0,1},{1,0},{2,3},{3,2},{4,5},{5,4},{6,7},{7,6},{8,9},{9,8},{10,11... | collective-permute-start | bytes 3145736 | tf_op jit(solution)/shard_map/ppermute | solution.py:293
  37.3 18.5 %all-to-all-start.2 = ((f32[16,136,128]{2,1,0:T(8,128)}), f32[16,136,128]{2,1,0:T(8,128)S(1)}, u32[]{:S(2)}, u32[]{:S(2)}) async-start(f32[16,136,128]{2,1,0:T(8,128)} %broadcast_in_dim.7), calls=%async_computation.2 | async-start | bytes 2228224 | tf_op jit(solution)/shard_map/all_to_all | solution.py:291
